TPU v7x, 8 devices: a whole 2x2x1 slice. The times are simulated.
8 devices in a mesh: pod: 1 (over z), dp: 2 (over y), tp: 4 (over x, core).
Axes of the slice: x: 2, y: 2, z: 1, core: 2. Of those that a mesh axis runs over, the one named last changes fastest.
Arguments:
- x_saved: bfloat16 [3072, 1024], P(('pod', 'dp'))
- h_saved: bfloat16 [3072, 1024], P(('pod', 'dp'))
- mean_one: float32 [3072], P(('pod', 'dp'))
- rstd_one: float32 [3072], P(('pod', 'dp'))
- mean_two: float32 [3072], P(('pod', 'dp'))
- rstd_two: float32 [3072], P(('pod', 'dp'))
- gain_one: bfloat16 [1024], replicated
- gain_two: bfloat16 [1024], replicated
- grad_y: bfloat16 [3072, 1024], P(('pod', 'dp'))
- w_qkv: bfloat16 [1024, 3, 16, 64], P(None, None, 'tp')
- w_proj: bfloat16 [16, 64, 1024], P('tp')
- w_up: bfloat16 [1024, 4096], P(None, 'tp')
- w_down: bfloat16 [4096, 1024], P('tp')
Outputs:
- output 1: bfloat16 [3072, 1024], P(('pod', 'dp'))
- output 2: bfloat16 [1024, 3, 16, 64], P('pod', None, 'tp')
- output 3: bfloat16 [16, 64, 1024], P(('pod', 'tp'))
- output 4: bfloat16 [1024, 4096], P('pod', 'tp')
- output 5: bfloat16 [4096, 1024], P(('pod', 'tp'))
All inputs are finite; a program needn't handle non-finite values.
Results may differ from a plain program's by a relative error of at most 0.017085.
Values are sent between devices in bfloat16 or wider.
A program may use at most 1 GiB of HBM per device.

v0:
```python
import math
import jax
import jax.numpy as jnp
from jax import lax
from jax.sharding import PartitionSpec as P

GELU_C = math.sqrt(2.0 / math.pi)


def layer_norm(row_vals, row_mean, row_rstd, gain_vec):
    x_hat = (row_vals.astype(jnp.float32) - row_mean[:, None]) * row_rstd[:, None]
    return x_hat, (x_hat * gain_vec.astype(jnp.float32)).astype(jnp.bfloat16)


def norm_back(d_norm, x_hat, row_rstd, gain_vec):
    scaled = d_norm * gain_vec.astype(jnp.float32)
    scaled_mean = jnp.mean(scaled, axis=-1, keepdims=True)
    proj_mean = jnp.mean(scaled * x_hat, axis=-1, keepdims=True)
    return row_rstd[:, None] * (scaled - scaled_mean - x_hat * proj_mean)


def gelu_pair(pre_act):
    pre_wide = pre_act.astype(jnp.float32)
    tanh_val = jnp.tanh(GELU_C * (pre_wide + 0.044715 * pre_wide * pre_wide * pre_wide))
    gelu_val = 0.5 * pre_wide * (1.0 + tanh_val)
    gelu_slope = 0.5 * (1.0 + tanh_val) + 0.5 * pre_wide * (1.0 - tanh_val * tanh_val) * GELU_C * (1.0 + 0.134145 * pre_wide * pre_wide)
    return gelu_val, gelu_slope


def causal_probs(q_heads, k_heads):
    tok_count = q_heads.shape[0]
    scores = jnp.einsum('qhe,khe->hqk', q_heads, k_heads, preferred_element_type=jnp.float32) * (q_heads.shape[-1] ** -0.5)
    row_ids = lax.broadcasted_iota(jnp.int32, (tok_count, tok_count), 0)
    col_ids = lax.broadcasted_iota(jnp.int32, (tok_count, tok_count), 1)
    scores = jnp.where(col_ids <= row_ids, scores, -1e30)
    shifted = jnp.exp(scores - jnp.max(scores, axis=-1, keepdims=True))
    return shifted / jnp.sum(shifted, axis=-1, keepdims=True)


def attn_grads(qkv_heads, prob_mat, prob_lo, d_attn):
    soft_scale = qkv_heads.shape[-1] ** -0.5
    dv_heads = jnp.einsum('hqk,qhe->khe', prob_lo, d_attn, preferred_element_type=jnp.float32).astype(jnp.bfloat16)
    d_probs = jnp.einsum('qhe,khe->hqk', d_attn, qkv_heads[:, 2], preferred_element_type=jnp.float32)
    d_scores = (prob_mat * (d_probs - jnp.sum(prob_mat * d_probs, axis=-1, keepdims=True)) * soft_scale).astype(jnp.bfloat16)
    dq_heads = jnp.einsum('hqk,khe->qhe', d_scores, qkv_heads[:, 1], preferred_element_type=jnp.float32).astype(jnp.bfloat16)
    dk_heads = jnp.einsum('hqk,qhe->khe', d_scores, qkv_heads[:, 0], preferred_element_type=jnp.float32).astype(jnp.bfloat16)
    return jnp.stack([dq_heads, dk_heads, dv_heads], axis=1)


def solution(mesh):
    row_spec = P(('pod', 'dp'), None)
    stat_spec = P(('pod', 'dp'))
    in_specs = (row_spec, row_spec, stat_spec, stat_spec, stat_spec, stat_spec, P(None), P(None), row_spec,
                P(None, None, 'tp', None), P('tp', None, None), P(None, 'tp'), P('tp', None))
    out_specs = (row_spec, P('pod', None, 'tp', None), P(('pod', 'tp'), None, None), P('pod', 'tp'), P(('pod', 'tp'), None))

    def local_step(x_saved, h_saved, mean_one, rstd_one, mean_two, rstd_two, gain_one, gain_two, grad_y, w_qkv, w_proj, w_up, w_down):
        hat_two, norm_two = layer_norm(h_saved, mean_two, rstd_two, gain_two)
        pre_act = jnp.dot(norm_two, w_up, preferred_element_type=jnp.float32).astype(jnp.bfloat16)
        gelu_val, gelu_slope = gelu_pair(pre_act)
        act_out = gelu_val.astype(jnp.bfloat16)
        d_act = lax.dot_general(grad_y, w_down, (((1,), (1,)), ((), ())), preferred_element_type=jnp.float32)
        d_pre = (d_act * gelu_slope).astype(jnp.bfloat16)
        grad_down = lax.dot_general(act_out, grad_y, (((0,), (0,)), ((), ())), preferred_element_type=jnp.float32)
        grad_up = lax.dot_general(norm_two, d_pre, (((0,), (0,)), ((), ())), preferred_element_type=jnp.float32)
        part_two = lax.dot_general(d_pre, w_up, (((1,), (1,)), ((), ())), preferred_element_type=jnp.float32).astype(jnp.bfloat16)
        d_norm_two = lax.psum(part_two, 'tp').astype(jnp.float32)
        d_mid = grad_y.astype(jnp.float32) + norm_back(d_norm_two, hat_two, rstd_two, gain_two)
        d_mid_lo = d_mid.astype(jnp.bfloat16)
        hat_one, norm_one = layer_norm(x_saved, mean_one, rstd_one, gain_one)
        qkv_heads = jnp.einsum('td,dche->tche', norm_one, w_qkv, preferred_element_type=jnp.float32).astype(jnp.bfloat16)
        prob_mat = causal_probs(qkv_heads[:, 0], qkv_heads[:, 1])
        prob_lo = prob_mat.astype(jnp.bfloat16)
        attn_out = jnp.einsum('hqk,khe->qhe', prob_lo, qkv_heads[:, 2], preferred_element_type=jnp.float32).astype(jnp.bfloat16)
        grad_proj = jnp.einsum('the,td->hed', attn_out, d_mid_lo, preferred_element_type=jnp.float32)
        d_attn = jnp.einsum('td,hed->the', d_mid_lo, w_proj, preferred_element_type=jnp.float32).astype(jnp.bfloat16)
        d_qkv = attn_grads(qkv_heads, prob_mat, prob_lo, d_attn)
        grad_qkv = jnp.einsum('td,tche->dche', norm_one, d_qkv, preferred_element_type=jnp.float32)
        part_one = jnp.einsum('tche,dche->td', d_qkv, w_qkv, preferred_element_type=jnp.float32).astype(jnp.bfloat16)
        d_norm_one = lax.psum(part_one, 'tp').astype(jnp.float32)
        grad_x = (d_mid + norm_back(d_norm_one, hat_one, rstd_one, gain_one)).astype(jnp.bfloat16)
        return (grad_x,
                lax.psum(grad_qkv, 'dp').astype(jnp.bfloat16),
                lax.psum(grad_proj, 'dp').astype(jnp.bfloat16),
                lax.psum(grad_up, 'dp').astype(jnp.bfloat16),
                lax.psum(grad_down, 'dp').astype(jnp.bfloat16))

    return jax.shard_map(local_step, mesh=mesh, in_specs=in_specs, out_specs=out_specs, check_vma=False)
```

profile of v0, /device:TPU:0, one launch (start us, length us, event | category | flops | bytes accessed | tf_op | source)
XLA Modules:
  0.0 577.2 jit_solution(12109388473567522202)
XLA Ops:
  7.2 0.0 all-reduce.5.cloned.1.call-start
  7.2 0.8 convert_element_type.103
  8.1 0.7 copy-done
  8.8 5.6 convolution_convert_fusion.1
  14.4 6.9 %fusion.27 = bf16[1536,1024]{1,0:T(8,128)(2,1)S(1)} fusion(bf16[1536,1024]{1,0:T(8,128)(2,1)S(1)} %convolution_convert_fusion.1, bf16[1536,1024]{1,0:T(8,128)(2,1)S(1)} %copy-done.8, bf16[1024,1024]{1,0:T(8,128)(2,1)S(1)} %copy-done.20), kind=kOutput, calls=%fused_computation.33 | convolution fusion | flops 3252682752 | bytes 11534336 | tf_op jit(solution)/shard_map/dot_general | solution.py:62
  21.4 1.7 copy-done.22
  23.1 4.9 convolution_convert_fusion
  28.0 0.0 all-reduce.5.cloned.1.call-update
  28.0 0.0 all-reduce.7.cloned.1.call-start
  28.0 2.1 iota_compare_fusion
  30.1 8.7 %fusion.87 = f32[1024,1024]{1,0:T(8,128)} fusion(bf16[1536,1024]{1,0:T(8,128)(2,1)} %copy-done.22, bf16[1536,1024]{1,0:T(8,128)(2,1)} %param.14, f32[1024]{0:T(1024)S(1)} %convert_element_type.103, f32[1536]{0:T(1024)S(1)} %copy-done.13, f32[1536]{0:T(1024)S(1)} %copy-done.14), kind=kOutput, calls=%fused_computation.93 | convolution fusion | flops 3229089792 | bytes 10502144 | tf_op jit(solution)/shard_map/dot_general | solution.py:65
  38.9 5.8 fusion.34
  44.7 2.9 fusion.89
  47.7 1.7 convert_element_type.113
  49.3 21.9 %exponential_reduce_fusion = (f32[4,1536]{1,0:T(4,128)S(1)}, f32[4,1536,1536]{1,2,0:T(8,128)}) fusion(pred[1536,1536]{0,1:T(8,128)(4,1)} %iota_compare_fusion, bf16[1536,3,4,64]{0,3,2,1:T(8,128)(2,1)} %convert_element_type.113), kind=kOutput, calls=%fused_computation.11 | convolution fusion | flops 1245709824 | bytes 41705472 | tf_op jit(solution)/shard_map/sub | solution.py:36
  71.2 22.5 %all-reduce.5.cloned.1.call-done = bf16[1536,1024]{1,0:T(8,128)(2,1)} async-done(((bf16[1536,1024]{1,0:T(8,128)(2,1)}), bf16[1536,1024]{1,0:T(8,128)(2,1)}) %all-reduce.5.cloned.1.call-update) | async-done | bytes 3145744 | tf_op jit(solution)/shard_map/psum | solution.py:67
  93.7 4.9 fusion.33
  98.7 4.5 multiply_add_fusion
  103.2 2.7 copy-done.2
  105.9 1.0 fusion.56
  106.9 16.0 %fusion.75 = f32[4,1536,1536]{1,2,0:T(8,128)} fusion(bf16[1536,4,64]{0,2,1:T(8,128)(2,1)S(1)} %fusion.56, bf16[1536,3,4,64]{0,3,2,1:T(8,128)(2,1)} %convert_element_type.113), kind=kOutput, calls=%fused_computation.77 | convolution fusion | flops 1207959552 | bytes 39321600 | tf_op jit(solution)/shard_map/qhe,khe->hqk/dot_general | solution.py:43
  122.9 19.5 %fusion.64 = bf16[1536,1,4,64]{0,3,2,1:T(8,128)(2,1)S(1)} fusion(bf16[1536,4,64]{0,2,1:T(8,128)(2,1)S(1)} %fusion.56, f32[4,1536]{1,0:T(4,128)S(1)} %get-tuple-element.13, pred[1536,1536]{0,1:T(8,128)(4,1)} %iota_compare_fusion, bf16[1536,3,4,64]{0,3,2,1:T(8,128)(2,1)} %convert_element_type.113), kind=kOutput, calls=%fused_computation.68 | convolution fusion | flops 2463505920 | bytes 5529600 | tf_op jit(solution)/shard_map/hqk,qhe->khe/dot_general | solution.py:42
  142.4 48.5 %fusion.67 = bf16[1536,1,4,64]{0,3,2,1:T(8,128)(2,1)S(1)} fusion(f32[4,1536,1536]{1,2,0:T(8,128)} %fusion.75, bf16[1536,3,4,64]{0,3,2,1:T(8,128)(2,1)} %convert_element_type.113, f32[4,1536,1536]{1,2,0:T(8,128)} %get-tuple-element.14, f32[4,1536]{1,0:T(4,128)S(1)} %get-tuple-element.13), kind=kOutput, calls=%fused_computation.69 | convolution fusion | flops 1274420736 | bytes 152616960 | tf_op jit(solution)/shard_map/hqk,qhe->khe/dot_general | solution.py:46
  190.9 48.1 %fusion.70 = bf16[1536,1,4,64]{0,3,2,1:T(8,128)(2,1)S(1)} fusion(f32[4,1536,1536]{1,2,0:T(8,128)} %fusion.75, bf16[1536,3,4,64]{0,3,2,1:T(8,128)(2,1)} %convert_element_type.113, f32[4,1536,1536]{1,2,0:T(8,128)} %get-tuple-element.14, f32[4,1536]{1,0:T(4,128)S(1)} %get-tuple-element.13), kind=kOutput, calls=%fused_computation.70 | convolution fusion | flops 1274420736 | bytes 152616960 | tf_op jit(solution)/shard_map/hqk,khe->qhe/dot_general | solution.py:45
  239.0 5.4 bitcast_convert_fusion
  244.5 1.7 pad_maximum_fusion
  246.1 17.3 %fusion.36 = f32[4,64,1024]{2,1,0:T(8,128)S(1)} fusion(f32[1536,1024]{1,0:T(8,128)} %copy-done.2, bf16[1536,3,4,64]{0,3,2,1:T(8,128)(2,1)} %convert_element_type.113, f32[4,1536,1536]{1,2,0:T(8,128)} %get-tuple-element.14, f32[4,1536]{1,0:T(4,128)S(1)} %get-tuple-element.13), kind=kOutput, calls=%fused_computation.54 | convolution fusion | flops 2034106368 | bytes 45899776 | tf_op jit(solution)/shard_map/the,td->hed/dot_general | solution.py:75
  263.5 0.0 all-reduce.7.cloned.1.call-update
  263.5 7.0 %fusion.88 = f32[1024,768]{0,1} fusion(bf16[1536,768]{0,1:T(8,128)(2,1)} %bitcast.77, bf16[1536,1024]{1,0:T(8,128)(2,1)} %param.13, f32[1024]{0:T(1024)S(1)} %copy-done.12, f32[1536]{0:T(1024)S(1)} %copy-done.16, f32[1536]{0:T(1024)S(1)} %copy-done.18), kind=kOutput, calls=%fused_computation.94 | convolution fusion | flops 2423783424 | bytes 8667136
  270.5 288.7 %all-reduce.8 = (bf16[1024,3,4,64]{0,3,2,1:T(8,128)(2,1)}, bf16[4,64,1024]{2,1,0:T(8,128)(2,1)}, bf16[1024,1024]{1,0:T(8,128)(2,1)}, bf16[1024,1024]{1,0:T(8,128)(2,1)}) all-reduce(f32[1024,3,4,64]{0,3,2,1:T(8,128)} %bitcast.76, f32[4,64,1024]{2,1,0:T(8,128)S(1)} %fusion.36, ...), channel_id=1, replica_groups=mesh['pod'=1,'dp'=2,'tp'=4] {'dp'}, use_global_device_ids=true, to_apply=%region_9.10 | all-reduce | flops 3145728 | bytes 18874368 | tf_op jit(solution)/shard_map/psum | solution.py:83
  559.2 5.0 fusion.32
  564.3 5.6 add_convert_fusion
  (52 shorter events, 0.1 us)
Async XLA Ops:
  7.2 1.6 copy-start
  7.2 86.5 %all-reduce.5.cloned.1.call-start = ((), (), s32[]{:S(2)}) async-start(), calls=%async_computation | async-start | bytes 6291456 | tf_op jit(solution)/shard_map/psum | solution.py:67
  8.8 5.6 copy-start.8
  8.8 5.6 copy-start.20
  14.4 6.9 %copy-start.23 = (bf16[1536,1024]{1,0:T(8,128)(2,1)}, bf16[1536,1024]{1,0:T(8,128)(2,1)S(1)}, u32[]{:S(2)}) copy-start(bf16[1536,1024]{1,0:T(8,128)(2,1)S(1)} %convolution_convert_fusion.1) | copy-start | bytes 9437188
  21.3 1.7 copy-start.22
  23.1 7.1 %copy-start.13 = (f32[1536]{0:T(1024)S(1)}, f32[1536]{0:T(1024)}, u32[]{:S(2)}) copy-start(f32[1536]{0:T(1024)} %param.17) | copy-start | bytes 18436
  23.1 7.1 %copy-start.14 = (f32[1536]{0:T(1024)S(1)}, f32[1536]{0:T(1024)}, u32[]{:S(2)}) copy-start(f32[1536]{0:T(1024)} %param.18) | copy-start | bytes 18436
  28.0 531.2 %all-reduce.7.cloned.1.call-start = ((), (), s32[]{:S(2)}) async-start(), calls=%async_computation.1 | async-start | bytes 6291456 | tf_op jit(solution)/shard_map/psum | solution.py:80
  30.1 8.7 %copy-start.9 = (bf16[1536,1024]{1,0:T(8,128)(2,1)S(1)}, bf16[1536,1024]{1,0:T(8,128)(2,1)}, u32[]{:S(2)}) copy-start(bf16[1536,1024]{1,0:T(8,128)(2,1)} %param.21) | copy-start | bytes 9437188
  30.1 8.7 %copy-start.24 = (bf16[1536,1024]{1,0:T(8,128)(2,1)S(1)}, bf16[1536,1024]{1,0:T(8,128)(2,1)}, u32[]{:S(2)}) copy-start(bf16[1536,1024]{1,0:T(8,128)(2,1)} %copy-done.23) | copy-start | bytes 9437188
  38.9 5.8 %copy-start.19 = (bf16[1024]{0:T(1024)(128)(2,1)S(1)}, bf16[1024]{0:T(1024)(128)(2,1)}, u32[]{:S(2)}) copy-start(bf16[1024]{0:T(1024)(128)(2,1)} %param.19) | copy-start | bytes 6148
  38.9 5.8 %copy-start.4 = (bf16[1536,1024]{1,0:T(8,128)(2,1)S(1)}, bf16[1536,1024]{1,0:T(8,128)(2,1)}, u32[]{:S(2)}) copy-start(bf16[1536,1024]{1,0:T(8,128)(2,1)} %param.13) | copy-start | bytes 9437188
  38.9 5.8 %copy-start.15 = (f32[1536]{0:T(1024)S(1)}, f32[1536]{0:T(1024)}, u32[]{:S(2)}) copy-start(f32[1536]{0:T(1024)} %param.15) | copy-start | bytes 18436
  38.9 5.8 %copy-start.17 = (f32[1536]{0:T(1024)S(1)}, f32[1536]{0:T(1024)}, u32[]{:S(2)}) copy-start(f32[1536]{0:T(1024)} %param.16) | copy-start | bytes 18436
  38.9 5.8 %copy-start.21 = (bf16[1024,3,4,64]{0,3,2,1:T(8,128)(2,1)S(1)}, bf16[1024,3,4,64]{0,3,2,1:T(8,128)(2,1)}, u32[]{:S(2)}) copy-start(bf16[1024,3,4,64]{0,3,2,1:T(8,128)(2,1)} %param.22) | copy-start | bytes 4718596
  44.7 2.9 copy-start.11
  93.7 4.9 copy-start.3
  93.7 4.9 copy-start.6
  98.6 7.3 %copy-start.10 = (bf16[4,64,1024]{2,1,0:T(8,128)(2,1)S(1)}, bf16[4,64,1024]{2,1,0:T(8,128)(2,1)}, u32[]{:S(2)}) copy-start(bf16[4,64,1024]{2,1,0:T(8,128)(2,1)} %param.23) | copy-start | bytes 1572868
  103.2 2.8 copy-start.2
  246.1 17.3 %copy-start.12 = (f32[1024]{0:T(1024)S(1)}, f32[1024]{0:T(1024)}, u32[]{:S(2)}) copy-start(f32[1024]{0:T(1024)} %copy-done.11) | copy-start | bytes 12292
  246.1 17.3 %copy-start.16 = (f32[1536]{0:T(1024)S(1)}, f32[1536]{0:T(1024)}, u32[]{:S(2)}) copy-start(f32[1536]{0:T(1024)} %param.15) | copy-start | bytes 18436
  246.1 17.4 %copy-start.18 = (f32[1536]{0:T(1024)S(1)}, f32[1536]{0:T(1024)}, u32[]{:S(2)}) copy-start(f32[1536]{0:T(1024)} %param.16) | copy-start | bytes 18436
  559.2 5.0 copy-start.5
  559.2 5.0 copy-start.7
  564.3 5.7 copy-start.1
Sparse Core Ops, SparseCore 0:
  28.1 65.5 all-reduce.4
  263.6 62.8 all-reduce.6
where the time goes:
time: 586 us; the launch traced here: 577 us
  blocking collectives  289 us (49%)
  matrix products  220 us (38%)
  other arithmetic  26.3 us (4%)
  waiting for transfers between devices  22.5 us (4%)
  between operations  14.8 us (3%)
    psum x1, blocking collectives, local_step(): lax.psum(grad_qkv, 'dp').astype(jnp.bfloat16)  289 us
    dot_general x1, matrix products, attn_grads(): jnp.einsum('hqk,qhe->khe', d_scores, qkv_heads[:, 0], preferred_element_t...  48.5 us
    dot_general x1, matrix products, attn_grads(): jnp.einsum('hqk,khe->qhe', d_scores, qkv_heads[:, 1], preferred_element_t...  48.1 us
    psum x1, waiting for transfers between devices, local_step(): d_norm_two = lax.psum(part_two, 'tp').astype(jnp.float32)  22.5 us
    sub x1, matrix products, causal_probs(): shifted = jnp.exp(scores - jnp.max(scores, axis=-1, keepdims=True))  21.9 us
    dot_general x1, matrix products, attn_grads(): jnp.einsum('hqk,qhe->khe', prob_lo, d_attn, preferred_element_type=jnp.fl...  19.5 us
    dot_general x1, matrix products, local_step(): jnp.einsum('the,td->hed', attn_out, d_mid_lo, preferred_element_type=jnp....  17.3 us
    dot_general x1, matrix products, attn_grads(): jnp.einsum('qhe,khe->hqk', d_attn, qkv_heads[:, 2], preferred_element_typ...  16 us
  transfers between devices with their start and end apart: 2, of which 1 were waited for; matrix products, arithmetic and copies ran while one was open for 9% of the time, Pallas kernels for 0%

commit v1 on v0

v1 whole, which is shorter than its diff:
```python
import functools
import math

import jax
import jax.numpy as jnp
from jax import lax
from jax.experimental import pallas as pl
from jax.experimental.pallas import tpu as pltpu
from jax.sharding import PartitionSpec as P

GELU_C = math.sqrt(2.0 / math.pi)
F32 = jnp.float32
BF16 = jnp.bfloat16
NT = (((1,), (1,)), ((), ()))
TN = (((0,), (0,)), ((), ()))
BLK = 256


def layer_norm(row_vals, row_mean, row_rstd, gain_vec):
    x_hat = (row_vals.astype(F32) - row_mean[:, None]) * row_rstd[:, None]
    return x_hat, (x_hat * gain_vec.astype(F32)).astype(BF16)


def norm_back(d_norm, x_hat, row_rstd, gain_vec):
    scaled = d_norm * gain_vec.astype(F32)
    scaled_mean = jnp.mean(scaled, axis=-1, keepdims=True)
    proj_mean = jnp.mean(scaled * x_hat, axis=-1, keepdims=True)
    return row_rstd[:, None] * (scaled - scaled_mean - x_hat * proj_mean)


def gelu_pair(pre_act):
    pre_wide = pre_act.astype(F32)
    tanh_val = jnp.tanh(GELU_C * (pre_wide + 0.044715 * pre_wide * pre_wide * pre_wide))
    gelu_val = 0.5 * pre_wide * (1.0 + tanh_val)
    gelu_slope = 0.5 * (1.0 + tanh_val) + 0.5 * pre_wide * (1.0 - tanh_val * tanh_val) * GELU_C * (1.0 + 0.134145 * pre_wide * pre_wide)
    return gelu_val, gelu_slope


def fold_rows(op, tile):
    return op(tile.reshape(tile.shape[0] // 8, 8, tile.shape[1]), axis=0)


def attn_kernel(q_ref, k_ref, v_ref, do_ref, ot_ref, dqkv_ref, s_ref, dp_ref, dk_ref, dv_ref, kt_ref, vt_ref):
    step = pl.program_id(0)
    last = pl.num_programs(0) - 1
    qi = last - step

    @pl.when(step == 0)
    def _():
        dk_ref[...] = jnp.zeros_like(dk_ref)
        dv_ref[...] = jnp.zeros_like(dv_ref)
        kt_ref[...] = k_ref[...].T
        vt_ref[...] = v_ref[...].T

    lane = lax.broadcasted_iota(jnp.int32, (BLK, 128), 1)
    q_wide = q_ref[...].astype(F32) * 0.125
    do_wide = do_ref[...].astype(F32)
    qs, dos = [], []
    for h in range(2):
        keep = (lane < 64) if h == 0 else (lane >= 64)
        qs.append(jnp.where(keep, q_wide, 0.0).astype(BF16))
        dos.append(jnp.where(keep, do_wide, 0.0).astype(BF16))

    def score(j, top, masked):
        rows = pl.ds(pl.multiple_of(j * BLK, BLK), BLK)
        k_blk = k_ref[rows, :]
        out = []
        for h in range(2):
            tile = lax.dot_general(k_blk, qs[h], NT, preferred_element_type=F32)
            if masked:
                key = lax.broadcasted_iota(jnp.int32, (BLK, BLK), 0)
                qry = lax.broadcasted_iota(jnp.int32, (BLK, BLK), 1)
                tile = jnp.where(key <= qry, tile, -1e30)
            s_ref[h, rows, :] = tile
            out.append(jnp.maximum(top[h], fold_rows(jnp.max, tile)))
        return tuple(out)

    low = jnp.full((8, BLK), -1e30, F32)
    top = score(qi, (low, low), True)
    top = lax.fori_loop(0, qi, lambda j, t: score(j, t, False), top)
    top = [jnp.max(t, axis=0, keepdims=True) for t in top]

    def expo(j, tot):
        rows = pl.ds(pl.multiple_of(j * BLK, BLK), BLK)
        out = []
        for h in range(2):
            tile = jnp.exp(s_ref[h, rows, :] - top[h])
            s_ref[h, rows, :] = tile
            out.append(tot[h] + fold_rows(jnp.sum, tile))
        return tuple(out)

    zero8 = jnp.zeros((8, BLK), F32)
    tot = lax.fori_loop(0, qi + 1, expo, (zero8, zero8))
    inv = [1.0 / jnp.sum(t, axis=0, keepdims=True) for t in tot]

    def third(j, carry):
        proj, o_acc = carry
        rows = pl.ds(pl.multiple_of(j * BLK, BLK), BLK)
        v_blk = v_ref[rows, :]
        proj_new, o_new = [], []
        dv_add = None
        for h in range(2):
            prob = s_ref[h, rows, :] * inv[h]
            s_ref[h, rows, :] = prob
            prob_lo = prob.astype(BF16)
            d_prob = lax.dot_general(v_blk, dos[h], NT, preferred_element_type=F32)
            dp_ref[h, rows, :] = d_prob
            proj_new.append(proj[h] + fold_rows(jnp.sum, prob * d_prob))
            term = jnp.dot(prob_lo, dos[h], preferred_element_type=F32)
            dv_add = term if h == 0 else dv_add + term
            o_new.append(o_acc[h] + jnp.dot(vt_ref[h * 64:(h + 1) * 64, rows], prob_lo, preferred_element_type=F32))
        dv_ref[rows, :] += dv_add
        return tuple(proj_new), tuple(o_new)

    zero_t = jnp.zeros((64, BLK), F32)
    proj, o_acc = lax.fori_loop(0, qi + 1, third, ((zero8, zero8), (zero_t, zero_t)))
    for h in range(2):
        ot_ref[h * 64:(h + 1) * 64, :] = o_acc[h].astype(BF16)
    proj = [jnp.sum(t, axis=0, keepdims=True) for t in proj]

    def fourth(j, dq_acc):
        rows = pl.ds(pl.multiple_of(j * BLK, BLK), BLK)
        dq_new = []
        dk_add = None
        for h in range(2):
            d_s = (s_ref[h, rows, :] * (dp_ref[h, rows, :] - proj[h])).astype(BF16)
            term = jnp.dot(d_s, qs[h], preferred_element_type=F32)
            dk_add = term if h == 0 else dk_add + term
            dq_new.append(dq_acc[h] + jnp.dot(kt_ref[h * 64:(h + 1) * 64, rows], d_s, preferred_element_type=F32))
        dk_ref[rows, :] += dk_add
        return tuple(dq_new)

    dq = lax.fori_loop(0, qi + 1, fourth, (zero_t, zero_t))
    dq = jnp.concatenate([d * 0.125 for d in dq], axis=0)
    rows = pl.ds(pl.multiple_of(qi * BLK, BLK), BLK)
    dqkv_ref[rows, 0:128] = dq.T.astype(BF16)

    @pl.when(step == last)
    def _():
        dqkv_ref[:, 128:256] = dk_ref[...].astype(BF16)
        dqkv_ref[:, 256:384] = dv_ref[...].astype(BF16)


def attn_pair(pair, qkv, d_attn):
    toks = qkv.shape[0]
    steps = toks // BLK
    return pl.pallas_call(
        attn_kernel,
        grid=(steps,),
        in_specs=[pl.BlockSpec((BLK, 128), lambda s: (steps - 1 - s, pair)),
                  pl.BlockSpec((toks, 128), lambda s: (0, 2 + pair)),
                  pl.BlockSpec((toks, 128), lambda s: (0, 4 + pair)),
                  pl.BlockSpec((BLK, 128), lambda s: (steps - 1 - s, pair))],
        out_specs=[pl.BlockSpec((128, BLK), lambda s: (0, steps - 1 - s)),
                   pl.BlockSpec((toks, 384), lambda s: (0, 0))],
        out_shape=[jax.ShapeDtypeStruct((128, toks), BF16), jax.ShapeDtypeStruct((toks, 384), BF16)],
        scratch_shapes=[pltpu.VMEM((2, toks, BLK), F32), pltpu.VMEM((2, toks, BLK), F32),
                        pltpu.VMEM((toks, 128), F32), pltpu.VMEM((toks, 128), F32),
                        pltpu.VMEM((128, toks), BF16), pltpu.VMEM((128, toks), BF16)],
        compiler_params=pltpu.CompilerParams(dimension_semantics=("arbitrary",), vmem_limit_bytes=40 << 20),
        cost_estimate=pl.CostEstimate(flops=16 * 10**9, bytes_accessed=4 << 20, transcendentals=0),
        name=f"attn_pair{pair}",
    )(qkv, qkv, qkv, d_attn)


def mlp_kernel(na_ref, da_ref, nb_ref, db_ref, wu_ref, wd_ref, pu_hbm, pd_hbm, gu_ref, gd_ref, au_ref, ad_ref, pu_ref, pd_ref, sem):
    step = pl.program_id(0)
    half = pl.num_programs(0) // 2
    load_u = pltpu.make_async_copy(pu_hbm, pu_ref, sem.at[0])
    load_d = pltpu.make_async_copy(pd_hbm, pd_ref, sem.at[1])

    @pl.when(step == 0)
    def _():
        load_u.start()
        load_d.start()
        au_ref[...] = jnp.zeros_like(au_ref)
        ad_ref[...] = jnp.zeros_like(ad_ref)

    def rows_of(n_ref, d_ref):
        n_two = n_ref[...]
        d_y = d_ref[...]
        pre = jnp.dot(n_two, wu_ref[...], preferred_element_type=F32).astype(BF16)
        act, slope = gelu_pair(pre)
        d_act = lax.dot_general(d_y, wd_ref[...], NT, preferred_element_type=F32)
        d_pre = (d_act * slope).astype(BF16)
        au_ref[...] += lax.dot_general(n_two, d_pre, TN, preferred_element_type=F32)
        ad_ref[...] += lax.dot_general(act.astype(BF16), d_y, TN, preferred_element_type=F32)

    @pl.when(step < half)
    def _():
        rows_of(na_ref, da_ref)

    @pl.when(step >= half)
    def _():
        rows_of(nb_ref, db_ref)

    @pl.when(step == pl.num_programs(0) - 1)
    def _():
        load_u.wait()
        load_d.wait()
        gu_ref[...] = (au_ref[...] + pu_ref[...]).astype(BF16)
        gd_ref[...] = (ad_ref[...] + pd_ref[...]).astype(BF16)


def mlp_grad(n_a, d_a, n_b, d_b, w_up, w_down, part_up, part_down):
    rows, dim = n_a.shape
    cols = w_up.shape[1]
    blk = 384
    half = rows // blk
    first = pl.BlockSpec((blk, dim), lambda s: (jnp.minimum(s, half - 1), 0))
    second = pl.BlockSpec((blk, dim), lambda s: (jnp.maximum(s - half, 0), 0))
    whole_up = pl.BlockSpec((dim, cols), lambda s: (0, 0))
    whole_down = pl.BlockSpec((cols, dim), lambda s: (0, 0))
    return pl.pallas_call(
        mlp_kernel,
        grid=(2 * half,),
        in_specs=[first, first, second, second, whole_up, whole_down,
                  pl.BlockSpec(memory_space=pl.ANY), pl.BlockSpec(memory_space=pl.ANY)],
        out_specs=[whole_up, whole_down],
        out_shape=[jax.ShapeDtypeStruct((dim, cols), BF16), jax.ShapeDtypeStruct((cols, dim), BF16)],
        scratch_shapes=[pltpu.VMEM((dim, cols), F32), pltpu.VMEM((cols, dim), F32),
                        pltpu.VMEM((dim, cols), F32), pltpu.VMEM((cols, dim), F32),
                        pltpu.SemaphoreType.DMA((2,))],
        compiler_params=pltpu.CompilerParams(dimension_semantics=("arbitrary",), vmem_limit_bytes=60 << 20),
        cost_estimate=pl.CostEstimate(flops=16 * 10**9, bytes_accessed=24 << 20, transcendentals=0),
        name="mlp_grad",
    )(n_a, d_a, n_b, d_b, w_up, w_down, part_up, part_down)


def solution(mesh):
    row_spec = P(('pod', 'dp'), None)
    stat_spec = P(('pod', 'dp'))
    in_specs = (row_spec, row_spec, stat_spec, stat_spec, stat_spec, stat_spec, P(None), P(None), row_spec,
                P(None, None, 'tp', None), P('tp', None, None), P(None, 'tp'), P('tp', None))
    out_specs = (row_spec, P('pod', None, 'tp', None), P(('pod', 'tp'), None, None), P('pod', 'tp'), P(('pod', 'tp'), None))
    swap_core = functools.partial(lax.ppermute, axis_name='tp', perm=[(0, 1), (1, 0), (2, 3), (3, 2)])
    swap_x = functools.partial(lax.ppermute, axis_name='tp', perm=[(0, 2), (2, 0), (1, 3), (3, 1)])
    swap_dp = functools.partial(lax.ppermute, axis_name='dp', perm=[(0, 1), (1, 0)])

    def take_half(arr, which):
        rows = arr.shape[0] // 2
        return lax.dynamic_slice_in_dim(arr, which * rows, rows, 0)

    def join_halves(mine, other, which):
        return jnp.concatenate([jnp.where(which == 0, mine, other), jnp.where(which == 0, other, mine)], axis=0)

    def local_step(x_saved, h_saved, mean_one, rstd_one, mean_two, rstd_two, gain_one, gain_two, grad_y, w_qkv, w_proj, w_up, w_down):
        core = lax.axis_index('tp') % 2
        dp_idx = lax.axis_index('dp')
        dim = x_saved.shape[1]

        def reduce_rows(part):
            chip = (take_half(part, core).astype(F32) + swap_core(take_half(part, 1 - core)).astype(F32)).astype(BF16)
            return chip.astype(F32) + swap_x(chip).astype(F32)

        hat_two, norm_two = layer_norm(h_saved, mean_two, rstd_two, gain_two)
        norm_y, dy_y = swap_dp(take_half(norm_two, core)), swap_dp(take_half(grad_y, core))
        norm_c, dy_c = swap_core(norm_y), swap_core(dy_y)

        pre_act = jnp.dot(norm_two, w_up, preferred_element_type=F32).astype(BF16)
        gelu_val, gelu_slope = gelu_pair(pre_act)
        act_out = gelu_val.astype(BF16)
        d_act = lax.dot_general(grad_y, w_down, NT, preferred_element_type=F32)
        d_pre = (d_act * gelu_slope).astype(BF16)
        part_two = lax.dot_general(d_pre, w_up, NT, preferred_element_type=F32).astype(BF16)
        part_down = lax.dot_general(act_out, grad_y, TN, preferred_element_type=F32)
        part_up = lax.dot_general(norm_two, d_pre, TN, preferred_element_type=F32)

        w_t = w_qkv.transpose(1, 2, 3, 0).reshape(-1, dim)
        hat_one, norm_one = layer_norm(x_saved, mean_one, rstd_one, gain_one)
        qkv = lax.dot_general(norm_one, w_t, NT, preferred_element_type=F32).astype(BF16)

        h_half, r_half = take_half(h_saved, core), take_half(rstd_two, core)
        hat_half, _ = layer_norm(h_half, take_half(mean_two, core), r_half, gain_two)
        d_mid = take_half(grad_y, core).astype(F32) + norm_back(reduce_rows(part_two), hat_half, r_half, gain_two)
        mid_half = d_mid.astype(BF16)
        d_mid_lo = join_halves(mid_half, swap_core(mid_half), core)

        w_o = w_proj.reshape(-1, dim)
        d_attn = lax.dot_general(d_mid_lo, w_o, NT, preferred_element_type=F32).astype(BF16)

        w_pairs = w_t.reshape(3, 2, 128, dim)
        halves, part_one = [], None
        for pair in range(2):
            o_t, d_qkv = attn_pair(pair, qkv, d_attn)
            g_qkv = lax.dot_general(d_qkv, norm_one, TN, preferred_element_type=F32)
            g_o = jnp.dot(o_t, d_mid_lo, preferred_element_type=F32)
            mine, theirs = [], []
            for g in (g_qkv, g_o):
                mine.append(take_half(g, dp_idx))
                theirs.append(take_half(g, 1 - dp_idx))
            mine, theirs = jnp.concatenate(mine, 0), jnp.concatenate(theirs, 0)
            summed = (mine + swap_dp(theirs)).astype(BF16)
            other = swap_dp(summed)
            halves.append((join_halves(summed[:192], other[:192], dp_idx), join_halves(summed[192:], other[192:], dp_idx)))
            w_p = w_pairs[:, pair].reshape(-1, dim)
            term = jnp.dot(d_qkv, w_p, preferred_element_type=F32)
            part_one = term if pair == 0 else part_one + term
        g_t = jnp.stack([h[0].reshape(3, 2, 64, dim) for h in halves], axis=1).reshape(3, 4, 64, dim)
        grad_qkv = g_t.transpose(3, 0, 1, 2)
        grad_proj = jnp.concatenate([h[1] for h in halves], axis=0).reshape(4, 64, dim)

        x_half, r_one = take_half(x_saved, core), take_half(rstd_one, core)
        hat_x, _ = layer_norm(x_half, take_half(mean_one, core), r_one, gain_one)
        gx_half = (d_mid + norm_back(reduce_rows(part_one.astype(BF16)), hat_x, r_one, gain_one)).astype(BF16)
        grad_x = join_halves(gx_half, swap_core(gx_half), core)

        grad_up, grad_down = mlp_grad(norm_y, dy_y, norm_c, dy_c, w_up, w_down, part_up, part_down)
        return grad_x, grad_qkv, grad_proj, grad_up, grad_down

    return jax.shard_map(local_step, mesh=mesh, in_specs=in_specs, out_specs=out_specs, check_vma=False)
```

time: 586 us -> 232 us (0.40); the launches traced: 577 us -> 229 us
  blocking collectives: 289 us -> 0 us
  matrix products: 220 us -> 49 us
  Pallas kernels: 0 us -> 67.3 us
  waiting for transfers between devices: 22.5 us -> 63.4 us
  starting transfers between devices: 0.08 us -> 14.2 us
  between operations: 14.8 us -> 1.57 us
  local copies, waits for them, and re-layouts: 5.27 us -> 11.9 us
    psum x1 -> x0, blocking collectives: 289 us -> none  [local_step(): lax.psum(grad_qkv, 'dp').astype(jnp.bfloat16)]
    dot_general x12 -> x13, matrix products: 188 us -> 49 us  [the longest x1 17.1 us: local_step(): part_down = lax.dot_general(act_out, grad_y, TN, preferred_element_type=F32)]
    pallas_call x0 -> x3, Pallas kernels: none -> 67.3 us  [the longest x2 42.2 us: attn_pair(): pl.pallas_call(attn_kernel, grid=(steps,), in_specs=[pl.BlockSpec((BLK, 1...]
    ppermute x0 -> x14, waiting for transfers between devices: none -> 63.4 us  [the longest x2 34.1 us: local_step(): summed = (mine + swap_dp(theirs)).astype(BF16)]
    psum x2 -> x0, waiting for transfers between devices: 22.5 us -> none  [the longest x1 22.5 us: local_step(): d_norm_two = lax.psum(part_two, 'tp').astype(jnp.float32)]
    sub x1 -> x0, matrix products: 21.9 us -> none  [causal_probs(): shifted = jnp.exp(scores - jnp.max(scores, axis=-1, keepdims=True))]
    ppermute x0 -> x14, starting transfers between devices: none -> 14.2 us  [the longest x2 4.33 us: reduce_rows(): return chip.astype(F32) + swap_x(chip).astype(F32)]
    unnamed x2 -> x0, matrix products: 9.93 us -> none
  transfers between devices with their start and end apart: 2 -> 14, of which waited for: 1 -> 4; matrix products, arithmetic and copies ran while one was open for 9% -> 23% of each run, Pallas kernels for 0% -> 29%
where the time goes in v1:
time: 232 us; the launch traced here: 229 us
  Pallas kernels  67.3 us (29%)
  waiting for transfers between devices  63.4 us (27%)
  matrix products  49 us (21%)
  other arithmetic  22 us (9%)
  starting transfers between devices  14.2 us (6%)
  local copies, waits for them, and re-layouts  11.9 us (5%)
    pallas_call x2, Pallas kernels, attn_pair(): pl.pallas_call(attn_kernel, grid=(steps,), in_specs=[pl.BlockSpec((BLK, 1...  42.2 us
    ppermute x2, waiting for transfers between devices, local_step(): summed = (mine + swap_dp(theirs)).astype(BF16)  34.1 us
    ppermute x2, waiting for transfers between devices, reduce_rows(): return chip.astype(F32) + swap_x(chip).astype(F32)  26.2 us
    pallas_call x1, Pallas kernels, mlp_grad(): pl.pallas_call(mlp_kernel, grid=(2 * half,), in_specs=[first, first, seco...  25.1 us
    dot_general x1, matrix products, local_step(): part_down = lax.dot_general(act_out, grad_y, TN, preferred_element_type=F32)  17.1 us
    dot_general x1, matrix products, local_step(): d_act = lax.dot_general(grad_y, w_down, NT, preferred_element_type=F32)  6.87 us
    dot_general x1, matrix products, local_step(): part_up = lax.dot_general(norm_two, d_pre, TN, preferred_element_type=F32)  5.15 us
    dot_general x1, matrix products, local_step(): lax.dot_general(d_pre, w_up, NT, preferred_element_type=F32).astype(BF16)  4.84 us
  transfers between devices with their start and end apart: 14, of which 4 were waited for; matrix products, arithmetic and copies ran while one was open for 23% of the time, Pallas kernels for 29%

profile of v1, /device:TPU:0, one launch (start us, length us, event | category | flops | bytes accessed | tf_op | source)
XLA Modules:
  0.0 229.4 jit_solution(14695705262062611276)
XLA Ops:
  1.4 2.7 %multiply_convert_fusion.1 = bf16[1536,1024]{1,0:T(8,128)(2,1)S(1)} fusion(bf16[1536,1024]{1,0:T(8,128)(2,1)} %param.14, f32[1024]{0:T(1024)S(1)} %convert_element_type.97, f32[1536]{0:T(1024)} %param.18, f32[1536]{0:T(1024)} %param.17), kind=kLoop, calls=%fused_computation.20 | loop fusion | flops 7864320 | bytes 6307840 | tf_op jit(solution)/shard_map/convert_element_type | solution.py:21
  4.1 1.6 copy-done.4
  5.8 3.6 %convolution_convert_fusion.1 = bf16[1536,1024]{1,0:T(8,128)(2,1)S(1)} fusion(bf16[1536,1024]{1,0:T(8,128)(2,1)S(1)} %multiply_convert_fusion.1, bf16[1024,1024]{1,0:T(8,128)(2,1)S(1)} %copy-done.16), kind=kOutput, calls=%fused_computation.22 | convolution fusion | flops 3222798336 | bytes 8388608 | tf_op jit(solution)/shard_map/dot_general | solution.py:260
  9.4 6.9 %fusion.6 = bf16[1536,1024]{1,0:T(8,128)(2,1)S(1)} fusion(bf16[1536,1024]{1,0:T(8,128)(2,1)S(1)} %convolution_convert_fusion.1, bf16[1536,1024]{1,0:T(8,128)(2,1)S(1)} %copy-done.7, bf16[1024,1024]{1,0:T(8,128)(2,1)S(1)} %copy-done.17), kind=kOutput, calls=%fused_computation.13 | convolution fusion | flops 3252682752 | bytes 11534336 | tf_op jit(solution)/shard_map/dot_general | solution.py:263
  16.3 1.8 copy-done.18
  18.1 4.8 %convolution_convert_fusion = bf16[1536,1024]{1,0:T(8,128)(2,1)} fusion(bf16[1536,1024]{1,0:T(8,128)(2,1)S(1)} %fusion.6, bf16[1024,1024]{1,0:T(8,128)(2,1)S(1)} %copy-done.16), kind=kOutput, calls=%fused_computation.21 | convolution fusion | flops 3222798336 | bytes 8388608 | tf_op jit(solution)/shard_map/dot_general | solution.py:265
  22.9 1.5 constant_dynamic-slice_fusion.10
  25.3 3.0 %collective-permute-done = bf16[768,1024]{1,0:T(8,128)(2,1)} collective-permute-done((bf16[768,1024]{1,0:T(8,128)(2,1)S(1)}, bf16[768,1024]{1,0:T(8,128)(2,1)}, u32[]{:S(2)}, u32[]{:S(2)}) %collective-permute-start) | collective-permute-done | bytes 1572896 | tf_op jit(solution)/shard_map/ppermute | solution.py:253
  28.4 2.6 %add_convert_fusion.3 = bf16[768,1024]{1,0:T(8,128)(2,1)S(1)} fusion(bf16[768,1024]{1,0:T(8,128)(2,1)} %collective-permute-done, bf16[1536,1024]{1,0:T(8,128)(2,1)} %convolution_convert_fusion, s32[]{:T(128)S(6)} %select_n.102), kind=kLoop, calls=%fused_computation.36 | loop fusion | flops 3145728 | bytes 4718596 | tf_op jit(solution)/shard_map/convert_element_type | solution.py:253
  31.0 2.8 %collective-permute-start.1 = (bf16[768,1024]{1,0:T(8,128)(2,1)S(1)}, bf16[768,1024]{1,0:T(8,128)(2,1)}, u32[]{:S(2)}, u32[]{:S(2)}) collective-permute-start(bf16[768,1024]{1,0:T(8,128)(2,1)S(1)} %add_convert_fusion.3), channel_id=1, source_target_pairs={{0,2},{2,0},{1,3},{3,1},{4,6},{6,4},{5,7},{7,5}} | collective-permute-start | bytes 4718600 | tf_op jit(solution)/shard_map/ppermute | solution.py:254
  35.1 1.5 collective-permute-start.10
  38.7 1.7 fusion.31
  42.3 26.2 %collective-permute-done.1 = bf16[768,1024]{1,0:T(8,128)(2,1)} collective-permute-done((bf16[768,1024]{1,0:T(8,128)(2,1)S(1)}, bf16[768,1024]{1,0:T(8,128)(2,1)}, u32[]{:S(2)}, u32[]{:S(2)}) %collective-permute-start.1) | collective-permute-done | bytes 1572896 | tf_op jit(solution)/shard_map/ppermute | solution.py:254
  68.6 2.6 %fusion.17 = (f32[768]{0:T(1024)S(1)}, f32[768]{0:T(1024)S(1)}) fusion(bf16[768,1024]{1,0:T(8,128)(2,1)} %collective-permute-done.1, bf16[768,1024]{1,0:T(8,128)(2,1)S(1)} %add_convert_fusion.3, f32[1024]{0:T(1024)S(1)} %convert_element_type.97, f32[768]{0:T(1024)S(1)} %dynamic_slice.62, f32[768]{0:T(1024)S(1)} %dynamic_slice.66, ...), kind=kLoop, calls=%fused_computation.42 | loop fusion | flops 7862784 | bytes 4734980 | tf_op jit(solution)/shard_map/reduce_sum | solution.py:26
  71.2 2.9 %fusion.30 = (bf16[768,1024]{1,0:T(8,128)(2,1)S(1)}, f32[768,1024]{1,0:T(8,128)S(1)}) fusion(f32[768]{0:T(1024)S(1)} %get-tuple-element.45, f32[768]{0:T(1024)S(1)} %dynamic_slice.66, bf16[1536,1024]{1,0:T(8,128)(2,1)S(1)} %copy-done.2, s32[]{:T(128)S(6)} %select_n.102, f32[768]{0:T(1024)S(1)} %get-tuple-element.46, f32[1024]{0:T(1024)S(1)} %convert_element_type.97, ...), kind=kLoop, calls=%fused_computation.91 | loop fusion | flops 11010048 | bytes 11026436 | tf_op jit(solution)/shard_map/convert_element_type | solution.py:276
  74.2 2.9 %convolution_convert_fusion.2.q_ref.k_ref.v_ref = bf16[1536,768]{1,0:T(8,128)(2,1)S(1)} fusion(bf16[1536,1024]{1,0:T(8,128)(2,1)S(1)} %multiply_convert_fusion, bf16[768,1024]{1,0:T(8,128)(2,1)S(1)} %bitcast.42), kind=kOutput, calls=%fused_computation.23 | convolution fusion | flops 2417098752 | bytes 7077888 | tf_op jit(solution)/shard_map/dot_general | solution.py:271
  77.1 17.1 %fusion.11.pd_hbm = f32[1024,1024]{1,0:T(8,128)} fusion(bf16[1536,1024]{1,0:T(8,128)(2,1)S(1)} %copy-done.9, bf16[1536,1024]{1,0:T(8,128)(2,1)S(1)} %copy-done.21), kind=kOutput, calls=%fused_computation.24 | convolution fusion | flops 3236954112 | bytes 10485760 | tf_op jit(solution)/shard_map/dot_general | solution.py:266
  95.7 21.1 %attn_pair0.1 = (bf16[128,1536]{1,0:T(8,128)(2,1)S(1)}, bf16[1536,384]{1,0:T(8,128)(2,1)S(1)}) custom-call(bf16[1536,768]{1,0:T(8,128)(2,1)S(1)} %convolution_convert_fusion.2.q_ref.k_ref.v_ref, bf16[1536,768]{1,0:T(8,128)(2,1)S(1)} %convolution_convert_fusion.2.q_ref.k_ref.v_ref, bf16[1536,768]{1,0:T(8,128)(2,1)S(1)} %convolution_convert_fusion.2.q_ref.k_ref.v_ref, ...), custom_call_target="tpu_custom_call" | custom-call | flops 16000000000 | bytes 4194304 | tf_op jit(solution)/shard_map/attn_pair0/pallas_call | solution.py:147
  116.8 21.1 %attn_pair1.1 = (bf16[128,1536]{1,0:T(8,128)(2,1)S(1)}, bf16[1536,384]{1,0:T(8,128)(2,1)S(1)}) custom-call(bf16[1536,768]{1,0:T(8,128)(2,1)S(1)} %convolution_convert_fusion.2.q_ref.k_ref.v_ref, bf16[1536,768]{1,0:T(8,128)(2,1)S(1)} %convolution_convert_fusion.2.q_ref.k_ref.v_ref, bf16[1536,768]{1,0:T(8,128)(2,1)S(1)} %convolution_convert_fusion.2.q_ref.k_ref.v_ref, ...), custom_call_target="tpu_custom_call" | custom-call | flops 16000000000 | bytes 4194304 | tf_op jit(solution)/shard_map/attn_pair1/pallas_call | solution.py:147
  138.4 1.8 fusion.32
  140.2 1.8 add_convert_fusion
  144.3 1.8 collective-permute-start.6
  148.9 1.5 collective-permute-start.4
  151.1 5.1 %fusion.35.pu_hbm = f32[1024,1024]{1,0:T(8,128)} fusion(bf16[1536,1024]{1,0:T(8,128)(2,1)S(1)} %copy-done.6, bf16[1536,1024]{1,0:T(8,128)(2,1)S(1)} %copy-done.19), kind=kOutput, calls=%fused_computation.96 | convolution fusion | flops 3221225472 | bytes 10485760 | tf_op jit(solution)/shard_map/dot_general | solution.py:267
  156.8 13.5 %collective-permute-done.6 = f32[256,1024]{1,0:T(8,128)S(1)} collective-permute-done((f32[256,1024]{1,0:T(8,128)S(1)}, f32[256,1024]{1,0:T(8,128)S(1)}, u32[]{:S(2)}, u32[]{:S(2)}) %collective-permute-start.6) | collective-permute-done | bytes 1048608 | tf_op jit(solution)/shard_map/ppermute | solution.py:293
  170.5 1.8 collective-permute-start.7
  172.3 20.5 %collective-permute-done.8 = f32[256,1024]{1,0:T(8,128)S(1)} collective-permute-done((f32[256,1024]{1,0:T(8,128)S(1)}, f32[256,1024]{1,0:T(8,128)S(1)}, u32[]{:S(2)}, u32[]{:S(2)}) %collective-permute-start.8) | collective-permute-done | bytes 1048608 | tf_op jit(solution)/shard_map/ppermute | solution.py:293
  193.0 1.8 collective-permute-start.9
  196.0 1.6 add_convert_fusion.1
  197.6 25.1 %mlp_grad.1 = (bf16[1024,1024]{1,0:T(8,128)(2,1)}, bf16[1024,1024]{1,0:T(8,128)(2,1)}) custom-call(bf16[768,1024]{1,0:T(8,128)(2,1)} %collective-permute-done.10.na_ref, bf16[768,1024]{1,0:T(8,128)(2,1)} %collective-permute-done.11.da_ref, bf16[768,1024]{1,0:T(8,128)(2,1)} %collective-permute-done.12.nb_ref, ...), custom_call_target="tpu_custom_call" | custom-call | flops 16000000000 | bytes 25165824 | tf_op jit(solution)/shard_map/mlp_grad/pallas_call | solution.py:214
  225.4 1.6 broadcast_select_fusion.1
  227.0 2.0 pad_maximum_fusion.1
  (98 shorter events, 19.3 us)
Async XLA Ops:
  0.6 94.0 %copy-start = (bf16[4,64,1024]{2,1,0:T(8,128)(2,1)S(1)}, bf16[4,64,1024]{2,1,0:T(8,128)(2,1)}, u32[]{:S(2)}) copy-start(bf16[4,64,1024]{2,1,0:T(8,128)(2,1)} %param.23) | copy-start | bytes 1572868
  1.4 4.4 %copy-start.16 = (bf16[1024,1024]{1,0:T(8,128)(2,1)S(1)}, bf16[1024,1024]{1,0:T(8,128)(2,1)}, u32[]{:S(2)}) copy-start(bf16[1024,1024]{1,0:T(8,128)(2,1)} %wu_ref.1) | copy-start | bytes 6291460
  5.8 3.6 %copy-start.7 = (bf16[1536,1024]{1,0:T(8,128)(2,1)S(1)}, bf16[1536,1024]{1,0:T(8,128)(2,1)}, u32[]{:S(2)}) copy-start(bf16[1536,1024]{1,0:T(8,128)(2,1)} %param.21) | copy-start | bytes 9437188
  5.8 3.6 %copy-start.17 = (bf16[1024,1024]{1,0:T(8,128)(2,1)S(1)}, bf16[1024,1024]{1,0:T(8,128)(2,1)}, u32[]{:S(2)}) copy-start(bf16[1024,1024]{1,0:T(8,128)(2,1)} %wd_ref.1) | copy-start | bytes 6291460
  9.4 6.9 %copy-start.20 = (bf16[1536,1024]{1,0:T(8,128)(2,1)}, bf16[1536,1024]{1,0:T(8,128)(2,1)S(1)}, u32[]{:S(2)}) copy-start(bf16[1536,1024]{1,0:T(8,128)(2,1)S(1)} %convolution_convert_fusion.1) | copy-start | bytes 9437188
  24.5 3.9 %collective-permute-start = (bf16[768,1024]{1,0:T(8,128)(2,1)S(1)}, bf16[768,1024]{1,0:T(8,128)(2,1)}, u32[]{:S(2)}, u32[]{:S(2)}) collective-permute-start(bf16[768,1024]{1,0:T(8,128)(2,1)S(1)} %constant_dynamic-slice_fusion.10), channel_id=1, source_target_pairs={{0,1},{1,0},{2,3},{3,2},{4,5},{5,4},{6,7},{7,6}} | collective-permute-start | bytes 4718600 | tf_op jit(solution)/shard_map/ppermute | solution.py:253
  25.3 8.5 %copy-start.5 = (bf16[1536,1024]{1,0:T(8,128)(2,1)S(1)}, bf16[1536,1024]{1,0:T(8,128)(2,1)}, u32[]{:S(2)}) copy-start(bf16[1536,1024]{1,0:T(8,128)(2,1)} %copy-done.4) | copy-start | bytes 9437188
  25.3 11.3 %copy-start.8 = (bf16[1536,1024]{1,0:T(8,128)(2,1)S(1)}, bf16[1536,1024]{1,0:T(8,128)(2,1)}, u32[]{:S(2)}) copy-start(bf16[1536,1024]{1,0:T(8,128)(2,1)} %param.21) | copy-start | bytes 9437188
  30.9 7.4 %copy-start.11 = (f32[1536]{0:T(1024)S(1)}, f32[1536]{0:T(1024)}, u32[]{:S(2)}) copy-start(f32[1536]{0:T(1024)} %param.18) | copy-start | bytes 18436
  31.0 7.5 %copy-start.12 = (f32[1536]{0:T(1024)S(1)}, f32[1536]{0:T(1024)}, u32[]{:S(2)}) copy-start(f32[1536]{0:T(1024)} %param.17) | copy-start | bytes 18436
  31.0 7.6 %copy-start.15 = (bf16[1024]{0:T(1024)(128)(2,1)S(1)}, bf16[1024]{0:T(1024)(128)(2,1)}, u32[]{:S(2)}) copy-start(bf16[1024]{0:T(1024)(128)(2,1)} %param.19) | copy-start | bytes 6148
  31.0 7.6 %copy-start.13 = (f32[1536]{0:T(1024)S(1)}, f32[1536]{0:T(1024)}, u32[]{:S(2)}) copy-start(f32[1536]{0:T(1024)} %param.16) | copy-start | bytes 18436
  31.0 7.6 %copy-start.14 = (f32[1536]{0:T(1024)S(1)}, f32[1536]{0:T(1024)}, u32[]{:S(2)}) copy-start(f32[1536]{0:T(1024)} %param.15) | copy-start | bytes 18436
  31.0 37.6 %collective-permute-start.1 = (bf16[768,1024]{1,0:T(8,128)(2,1)S(1)}, bf16[768,1024]{1,0:T(8,128)(2,1)}, u32[]{:S(2)}, u32[]{:S(2)}) collective-permute-start(bf16[768,1024]{1,0:T(8,128)(2,1)S(1)} %add_convert_fusion.3), channel_id=1, source_target_pairs={{0,2},{2,0},{1,3},{3,1},{4,6},{6,4},{5,7},{7,5}} | collective-permute-start | bytes 4718600 | tf_op jit(solution)/shard_map/ppermute | solution.py:254
  35.1 121.2 %collective-permute-start.10 = (bf16[768,1024]{1,0:T(8,128)(2,1)}, bf16[768,1024]{1,0:T(8,128)(2,1)}, u32[]{:S(2)}, u32[]{:S(2)}) collective-permute-start(bf16[768,1024]{1,0:T(8,128)(2,1)} %constant_dynamic-slice_fusion), channel_id=1, source_target_pairs={{0,4},{4,0},{1,5},{5,1},{2,6},{6,2},{3,7},{7,3}} | collective-permute-start | bytes 4718600 | tf_op jit(solution)/shard_map/ppermute | solution.py:257
  37.9 118.4 %collective-permute-start.11 = (bf16[768,1024]{1,0:T(8,128)(2,1)}, bf16[768,1024]{1,0:T(8,128)(2,1)}, u32[]{:S(2)}, u32[]{:S(2)}) collective-permute-start(bf16[768,1024]{1,0:T(8,128)(2,1)} %constant_dynamic-slice_fusion.11), channel_id=1, source_target_pairs={{0,4},{4,0},{1,5},{5,1},{2,6},{6,2},{3,7},{7,3}} | collective-permute-start | bytes 4718600 | tf_op jit(solution)/shard_map/ppermute | solution.py:257
  41.1 27.5 %copy-start.2 = (bf16[1536,1024]{1,0:T(8,128)(2,1)S(1)}, bf16[1536,1024]{1,0:T(8,128)(2,1)}, u32[]{:S(2)}) copy-start(bf16[1536,1024]{1,0:T(8,128)(2,1)} %param.14) | copy-start | bytes 9437188
  42.3 28.9 %copy-start.9 = (bf16[1536,1024]{1,0:T(8,128)(2,1)S(1)}, bf16[1536,1024]{1,0:T(8,128)(2,1)}, u32[]{:S(2)}) copy-start(bf16[1536,1024]{1,0:T(8,128)(2,1)} %param.21) | copy-start | bytes 9437188
  71.2 3.0 %copy-start.10 = (bf16[1024,3,4,64]{0,3,2,1:T(8,128)(2,1)S(1)}, bf16[1024,3,4,64]{0,3,2,1:T(8,128)(2,1)}, u32[]{:S(2)}) copy-start(bf16[1024,3,4,64]{0,3,2,1:T(8,128)(2,1)} %param.22) | copy-start | bytes 4718596
  74.1 20.1 %collective-permute-start.2 = (bf16[768,1024]{1,0:T(8,128)(2,1)S(1)}, bf16[768,1024]{1,0:T(8,128)(2,1)S(1)}, u32[]{:S(2)}, u32[]{:S(2)}) collective-permute-start(bf16[768,1024]{1,0:T(8,128)(2,1)S(1)} %get-tuple-element.21), channel_id=1, source_target_pairs={{0,1},{1,0},{2,3},{3,2},{4,5},{5,4},{6,7},{7,6}} | collective-permute-start | bytes 4718600 | tf_op jit(solution)/shard_map/ppermute | solution.py:277
  74.2 2.9 %copy-start.21 = (bf16[1536,1024]{1,0:T(8,128)(2,1)S(1)}, bf16[1536,1024]{1,0:T(8,128)(2,1)}, u32[]{:S(2)}) copy-start(bf16[1536,1024]{1,0:T(8,128)(2,1)} %copy-done.20) | copy-start | bytes 9437188
  142.2 6.1 %collective-permute-start.3 = (bf16[768,1024]{1,0:T(8,128)(2,1)S(1)}, bf16[768,1024]{1,0:T(8,128)(2,1)S(1)}, u32[]{:S(2)}, u32[]{:S(2)}) collective-permute-start(bf16[768,1024]{1,0:T(8,128)(2,1)S(1)} %constant_dynamic-slice_fusion.9), channel_id=1, source_target_pairs={{0,1},{1,0},{2,3},{3,2},{4,5},{5,4},{6,7},{7,6}} | collective-permute-start | bytes 4718600 | tf_op jit(solution)/shard_map/ppermute | solution.py:253
  144.3 26.1 %collective-permute-start.6 = (f32[256,1024]{1,0:T(8,128)S(1)}, f32[256,1024]{1,0:T(8,128)S(1)}, u32[]{:S(2)}, u32[]{:S(2)}) collective-permute-start(f32[256,1024]{1,0:T(8,128)S(1)} %pad_maximum_fusion.3), channel_id=1, source_target_pairs={{0,4},{4,0},{1,5},{5,1},{2,6},{6,2},{3,7},{7,3}} | collective-permute-start | bytes 3145736 | tf_op jit(solution)/shard_map/ppermute | solution.py:293
  148.2 2.9 %copy-start.6 = (bf16[1536,1024]{1,0:T(8,128)(2,1)S(1)}, bf16[1536,1024]{1,0:T(8,128)(2,1)}, u32[]{:S(2)}) copy-start(bf16[1536,1024]{1,0:T(8,128)(2,1)} %copy-done.4) | copy-start | bytes 9437188
  148.2 2.9 %copy-start.19 = (bf16[1536,1024]{1,0:T(8,128)(2,1)S(1)}, bf16[1536,1024]{1,0:T(8,128)(2,1)}, u32[]{:S(2)}) copy-start(bf16[1536,1024]{1,0:T(8,128)(2,1)} %copy-done.18) | copy-start | bytes 9437188
  148.9 45.8 %collective-permute-start.4 = (bf16[768,1024]{1,0:T(8,128)(2,1)S(1)}, bf16[768,1024]{1,0:T(8,128)(2,1)S(1)}, u32[]{:S(2)}, u32[]{:S(2)}) collective-permute-start(bf16[768,1024]{1,0:T(8,128)(2,1)S(1)} %add_convert_fusion.2), channel_id=1, source_target_pairs={{0,2},{2,0},{1,3},{3,1},{4,6},{6,4},{5,7},{7,5}} | collective-permute-start | bytes 4718600 | tf_op jit(solution)/shard_map/ppermute | solution.py:254
  150.6 42.2 %collective-permute-start.8 = (f32[256,1024]{1,0:T(8,128)S(1)}, f32[256,1024]{1,0:T(8,128)S(1)}, u32[]{:S(2)}, u32[]{:S(2)}) collective-permute-start(f32[256,1024]{1,0:T(8,128)S(1)} %pad_maximum_fusion.4), channel_id=1, source_target_pairs={{0,4},{4,0},{1,5},{5,1},{2,6},{6,2},{3,7},{7,3}} | collective-permute-start | bytes 3145736 | tf_op jit(solution)/shard_map/ppermute | solution.py:293
  156.3 41.3 %collective-permute-start.12 = (bf16[768,1024]{1,0:T(8,128)(2,1)}, bf16[768,1024]{1,0:T(8,128)(2,1)}, u32[]{:S(2)}, u32[]{:S(2)}) collective-permute-start(bf16[768,1024]{1,0:T(8,128)(2,1)} %collective-permute-done.10.na_ref), channel_id=1, source_target_pairs={{0,1},{1,0},{2,3},{3,2},{4,5},{5,4},{6,7},{7,6}} | collective-permute-start | bytes 4718600 | tf_op jit(solution)/shard_map/ppermute | solution.py:258
  156.3 41.3 %collective-permute-start.13 = (bf16[768,1024]{1,0:T(8,128)(2,1)}, bf16[768,1024]{1,0:T(8,128)(2,1)}, u32[]{:S(2)}, u32[]{:S(2)}) collective-permute-start(bf16[768,1024]{1,0:T(8,128)(2,1)} %collective-permute-done.11.da_ref), channel_id=1, source_target_pairs={{0,1},{1,0},{2,3},{3,2},{4,5},{5,4},{6,7},{7,6}} | collective-permute-start | bytes 4718600 | tf_op jit(solution)/shard_map/ppermute | solution.py:258
  170.5 52.3 %collective-permute-start.7 = (bf16[256,1024]{1,0:T(8,128)(2,1)S(1)}, bf16[256,1024]{1,0:T(8,128)(2,1)S(1)}, u32[]{:S(2)}, u32[]{:S(2)}) collective-permute-start(bf16[256,1024]{1,0:T(8,128)(2,1)S(1)} %fusion.19), channel_id=1, source_target_pairs={{0,4},{4,0},{1,5},{5,1},{2,6},{6,2},{3,7},{7,3}} | collective-permute-start | bytes 1572872 | tf_op jit(solution)/shard_map/ppermute | solution.py:294
  193.0 29.9 %collective-permute-start.9 = (bf16[256,1024]{1,0:T(8,128)(2,1)S(1)}, bf16[256,1024]{1,0:T(8,128)(2,1)S(1)}, u32[]{:S(2)}, u32[]{:S(2)}) collective-permute-start(bf16[256,1024]{1,0:T(8,128)(2,1)S(1)} %fusion.20), channel_id=1, source_target_pairs={{0,4},{4,0},{1,5},{5,1},{2,6},{6,2},{3,7},{7,3}} | collective-permute-start | bytes 1572872 | tf_op jit(solution)/shard_map/ppermute | solution.py:294
  197.6 27.8 %collective-permute-start.5 = (bf16[768,1024]{1,0:T(8,128)(2,1)S(1)}, bf16[768,1024]{1,0:T(8,128)(2,1)}, u32[]{:S(2)}, u32[]{:S(2)}) collective-permute-start(bf16[768,1024]{1,0:T(8,128)(2,1)S(1)} %add_convert_fusion.1), channel_id=1, source_target_pairs={{0,1},{1,0},{2,3},{3,2},{4,5},{5,4},{6,7},{7,6}} | collective-permute-start | bytes 4718600 | tf_op jit(solution)/shard_map/ppermute | solution.py:306
  (4 other events, 7.8 us)
